TPU v7x, 32 devices: a 4x4x1 block of a 4x4x8 slice. The times are simulated.
32 devices in a mesh: dp: 1 (over z), tp: 32 (over x, y, core).
Axes of the slice: x: 4, y: 4, z: 1, core: 2. Of those that a mesh axis runs over, the one named last changes fastest.
The devices are a block of a 4x4x8 slice.
Arguments:
- x: bfloat16 [2048, 2048], P('dp')
- dy: bfloat16 [2048, 2048], P('dp')
- gate: bfloat16 [2048, 16384], P('dp', 'tp')
- up: bfloat16 [2048, 16384], P('dp', 'tp')
- w_gate: bfloat16 [2048, 16384], P(None, 'tp')
- w_up: bfloat16 [2048, 16384], P(None, 'tp')
- w_down: bfloat16 [16384, 2048], P('tp')
Outputs:
- output 1: bfloat16 [2048, 2048], P('dp')
- output 2: bfloat16 [2048, 16384], P('dp', 'tp')
- output 3: bfloat16 [2048, 16384], P('dp', 'tp')
- output 4: bfloat16 [16384, 2048], P(('dp', 'tp'))
All inputs are finite; a program needn't handle non-finite values.
Results may differ from a plain program's by a relative error of at most 0.012.
Values are sent between devices in bfloat16 or wider.
A program may use at most 768 MiB of HBM per device.

v0:
```python
import jax
import jax.numpy as jnp
from jax import lax
from jax.sharding import PartitionSpec as P


def act(gate, up):
    return jax.nn.gelu(gate) * up


def solution(mesh):
    def step(x, dy, gate, up, w_gate, w_up, w_down):
        hidden, back = jax.vjp(act, gate.astype(jnp.float32), up.astype(jnp.float32))
        d_hidden = jnp.dot(dy, w_down.T, preferred_element_type=jnp.float32)
        d_gate, d_up = (g.astype(jnp.bfloat16) for g in back(d_hidden))
        term = jnp.dot(d_gate, w_gate.T, preferred_element_type=jnp.float32) + jnp.dot(d_up, w_up.T, preferred_element_type=jnp.float32)
        dx = lax.psum(term.astype(jnp.bfloat16), "tp")
        dw_gate = jnp.dot(x.T, d_gate, preferred_element_type=jnp.float32)
        dw_up = jnp.dot(x.T, d_up, preferred_element_type=jnp.float32)
        dw_down = jnp.dot(hidden.astype(jnp.bfloat16).T, dy, preferred_element_type=jnp.float32)
        return dx, *(g.astype(jnp.bfloat16) for g in (dw_gate, dw_up, dw_down))

    tokens, columns, rows = P("dp", None), P(None, "tp"), P("tp", None)
    return jax.shard_map(
        step,
        mesh=mesh,
        in_specs=(tokens, tokens, P("dp", "tp"), P("dp", "tp"), columns, columns, rows),
        out_specs=(tokens, P("dp", "tp"), P("dp", "tp"), P(("dp", "tp"), None)),
        check_vma=False,
    )
```

profile of v0, /device:TPU:97, one launch (start us, length us, event | category | flops | bytes accessed | tf_op | source)
XLA Modules:
  0.0 176.3 jit_solution(10799273143721931049)
XLA Ops:
  7.2 0.0 copy-start
  7.2 0.1 all-reduce.2.cloned.1.call-start
  7.3 14.6 %fusion.4 = (bf16[2048,512]{1,0:T(8,128)(2,1)S(1)}, f32[2048,512]{1,0:T(8,128)}) fusion(bf16[2048,512]{1,0:T(8,128)(2,1)} %param.9, bf16[2048,512]{1,0:T(8,128)(2,1)} %param.10, bf16[2048,2048]{1,0:T(8,128)(2,1)} %param.8, bf16[512,2048]{1,0:T(8,128)(2,1)} %param.13), kind=kOutput, calls=%fused_computation.12 | convolution fusion | flops 4319084544 | bytes 20971520 | tf_op jit(solution)/shard_map/dot_general | solution.py:14
  21.8 0.0 copy-start.2
  21.8 0.0 copy-done
  21.8 8.3 %fusion.21 = f32[2048,2048]{1,0:T(8,128)} fusion(bf16[2048,512]{1,0:T(8,128)(2,1)S(1)} %get-tuple-element.8, bf16[2048,512]{1,0:T(8,128)(2,1)S(1)} %copy-done), kind=kOutput, calls=%fused_computation.32 | convolution fusion | flops 4294967296 | bytes 20971520 | tf_op jit(solution)/shard_map/dot_general | solution.py:16
  30.2 0.0 copy-done.2
  30.2 16.9 %add_convert_fusion = bf16[2048,2048]{1,0:T(8,128)(2,1)} fusion(f32[2048,2048]{1,0:T(8,128)} %fusion.21, bf16[2048,512]{1,0:T(8,128)(2,1)} %param.12, f32[2048,512]{1,0:T(8,128)} %get-tuple-element.9, bf16[2048,512]{1,0:T(8,128)(2,1)} %param.9), kind=kOutput, calls=%fused_computation | convolution fusion | flops 4314890240 | bytes 33554432 | tf_op jit(solution)/shard_map/dot_general | solution.py:16
  47.1 0.1 all-reduce.2.cloned.1.call-update
  47.1 8.6 %fusion.10 = bf16[2048,512]{0,1:T(8,128)(2,1)S(1)} fusion(bf16[2048,512]{1,0:T(8,128)(2,1)} %copy-done.2, bf16[2048,2048]{1,0:T(8,128)(2,1)} %param.7), kind=kOutput, calls=%fused_computation.22 | convolution fusion | flops 4296015872 | bytes 12582912 | tf_op jit(solution)/shard_map/dot_general | solution.py:18
  55.7 2.5 %copy.11 = bf16[2048,512]{1,0:T(8,128)(2,1)} copy(bf16[2048,512]{0,1:T(8,128)(2,1)S(1)} %fusion.10) | data formatting | bytes 4194304
  58.2 10.6 %fusion.11 = bf16[2048,512]{0,1:T(8,128)(2,1)S(1)} fusion(bf16[2048,2048]{1,0:T(8,128)(2,1)} %param.7, f32[2048,512]{1,0:T(8,128)} %get-tuple-element.9, bf16[2048,512]{1,0:T(8,128)(2,1)} %param.9), kind=kOutput, calls=%fused_computation.23 | convolution fusion | flops 4307550208 | bytes 16777216 | tf_op jit(solution)/shard_map/dot_general | solution.py:19
  68.9 2.5 %copy.12 = bf16[2048,512]{1,0:T(8,128)(2,1)} copy(bf16[2048,512]{0,1:T(8,128)(2,1)S(1)} %fusion.11) | data formatting | bytes 4194304
  71.4 11.6 %convolution_convert_fusion = bf16[512,2048]{1,0:T(8,128)(2,1)} fusion(bf16[2048,2048]{1,0:T(8,128)(2,1)} %param.8, bf16[2048,512]{1,0:T(8,128)(2,1)} %param.10, bf16[2048,512]{1,0:T(8,128)(2,1)} %param.9), kind=kOutput, calls=%fused_computation.19 | convolution fusion | flops 4308598784 | bytes 14680064 | tf_op jit(solution)/shard_map/dot_general | solution.py:20
  83.0 77.8 %all-reduce.2.cloned.1.call-done = bf16[2048,2048]{1,0:T(8,128)(2,1)} async-done(((bf16[2048,2048]{1,0:T(8,128)(2,1)}), bf16[2048,2048]{1,0:T(8,128)(2,1)}) %all-reduce.2.cloned.1.call-update) | async-done | bytes 8388624 | tf_op jit(solution)/shard_map/psum | solution.py:17
  160.8 0.0 copy-start.1
  160.8 8.6 %copy.14 = bf16[2048,2048]{1,0:T(8,128)(2,1)} copy(bf16[2048,2048]{1,0:T(8,128)(2,1)} %all-reduce.2.cloned.1.call-done) | data formatting | bytes 16777216
  169.4 0.0 copy-done.1
Async XLA Ops:
  7.2 14.7 %copy-start = (bf16[2048,512]{1,0:T(8,128)(2,1)S(1)}, bf16[2048,512]{1,0:T(8,128)(2,1)}, u32[]{:S(2)}) copy-start(bf16[2048,512]{1,0:T(8,128)(2,1)} %param.11) | copy-start | bytes 6291460
  7.2 153.6 %all-reduce.2.cloned.1.call-start = ((), (), s32[]{:S(2)}) async-start(), calls=%async_computation | async-start | bytes 16777216 | tf_op jit(solution)/shard_map/psum | solution.py:17
  21.8 8.3 %copy-start.2 = (bf16[2048,512]{1,0:T(8,128)(2,1)}, bf16[2048,512]{1,0:T(8,128)(2,1)S(1)}, u32[]{:S(2)}) copy-start(bf16[2048,512]{1,0:T(8,128)(2,1)S(1)} %get-tuple-element.8) | copy-start | bytes 6291460
  160.8 8.6 %copy-start.1 = (bf16[2048,512]{1,0:T(8,128)(2,1)S(1)}, bf16[2048,512]{1,0:T(8,128)(2,1)}, u32[]{:S(2)}) copy-start(bf16[2048,512]{1,0:T(8,128)(2,1)} %param.11) | copy-start | bytes 6291460
Sparse Core Ops, SparseCore 0:
  47.3 113.5 all-reduce.1
where the time goes:
time: 176 us
  waiting for transfers between devices  77.9 us (44%)
  matrix products  70.6 us (40%)
  between operations  14.1 us (8%)
  local copies, waits for them, and re-layouts  13.6 us (8%)
    psum x1, waiting for transfers between devices, step(): dx = lax.psum(term.astype(jnp.bfloat16), 'tp')  77.8 us
    dot_general x1, matrix products, step(): jnp.dot(d_up, w_up.T, preferred_element_type=jnp.float32)  16.9 us
    dot_general x1, matrix products, step(): d_hidden = jnp.dot(dy, w_down.T, preferred_element_type=jnp.float32)  14.6 us
    unnamed x9, local copies, waits for them, and re-layouts  13.6 us
    dot_general x1, matrix products, step(): jnp.dot(hidden.astype(jnp.bfloat16).T, dy, preferred_element_type=jnp.flo...  11.6 us
    dot_general x1, matrix products, step(): dw_up = jnp.dot(x.T, d_up, preferred_element_type=jnp.float32)  10.6 us
    dot_general x1, matrix products, step(): dw_gate = jnp.dot(x.T, d_gate, preferred_element_type=jnp.float32)  8.59 us
    dot_general x1, matrix products, step(): jnp.dot(d_gate, w_gate.T, preferred_element_type=jnp.float32)  8.33 us
  transfers between devices with their start and end apart: 1, of which 1 were waited for; matrix products, arithmetic and copies ran while one was open for 20% of the time, Pallas kernels for 0%

commit v1 on v0

v1 whole, which is shorter than its diff:
```python
import functools
import math

import jax
import jax.numpy as jnp
from jax import lax
from jax.experimental import pallas as pl
from jax.experimental.pallas import tpu as pltpu
from jax.sharding import PartitionSpec as P

MESH = pl.DeviceIdType.MESH
CHUNK = 256
BF16, F32 = jnp.bfloat16, jnp.float32
COPIES = 21
SLOTS = 5


def dot(a, b, ca, cb):
    return lax.dot_general(a, b, (((ca,), (cb,)), ((), ())), preferred_element_type=F32)


def kernel(side, x, dy, gate, up, wg, wu, wd, dx, dwg, dwu, dwd,
           wdv, wv, dyv, gu, hid, xs, own, sT, rT, sA, rA, sB, rB, sC, rC, sD, rD, wsem, lsem, xsem, ssem, rsem):
    rows, d = dx.shape
    f = wd.shape[0]
    m = min(CHUNK, rows)
    n = rows // m
    half, q = m // 2, m // 8
    ch, cq, ce = d // 2, d // 4, d // 8
    units, uw = n, d // n

    me = lax.axis_index("tp")
    core = lax.rem(me, 2)
    chip = me // 2
    px, py = chip // side, lax.rem(chip, side)
    p1 = px + core * (py - px)
    p2 = py + core * (px - py)

    def at(a, b):
        return ((1 - core) * (a * side + b) + core * (b * side + a)) * 2 + core

    def turn(p, k):
        return lax.rem(p + k, side)

    r1, o1, l1 = turn(p1, 1), turn(p1, 2), turn(p1, 3)
    r2, o2, l2 = turn(p2, 1), turn(p2, 2), turn(p2, 3)
    partner = me + 1 - 2 * core
    first = (at(r1, p2), at(l1, p2))
    second = (at(p1, r2), at(p1, l2))

    barrier = pltpu.get_barrier_semaphore()
    for dev in (partner, *first, *second):
        pl.semaphore_signal(barrier, inc=1, device_id={"tp": dev}, device_id_type=MESH)

    def load(src, dst, sem):
        return pltpu.make_async_copy(src, dst, sem)

    def chunk_loads(c):
        r = pl.ds(pl.multiple_of(c * m, m), m)
        return (
            load(dy.at[r], dyv.at[r], lsem.at[c, 0]),
            load(gate.at[r], gu.at[r, pl.ds(0, f)], lsem.at[c, 1]),
            load(up.at[r], gu.at[r, pl.ds(f, f)], lsem.at[c, 2]),
        )

    def unit_load(j, slot):
        return load(x.at[:, pl.ds(pl.multiple_of(j * uw, uw), uw)], xs.at[slot], xsem.at[slot])

    load_wd = load(wd, wdv, wsem.at[0])
    load_wg = load(wg, wv.at[:, pl.ds(0, f)], wsem.at[1])
    load_wu = load(wu, wv.at[:, pl.ds(f, f)], wsem.at[2])
    load_wd.start()
    for cp in chunk_loads(0):
        cp.start()
    load_wg.start()
    load_wu.start()
    for c in range(1, min(3, n)):
        for cp in chunk_loads(c):
            cp.start()
    pl.semaphore_wait(barrier, 5)

    def send(c, k, src, dst, dev):
        return pltpu.make_async_remote_copy(
            src, dst, ssem.at[c, k], rsem.at[c, k], device_id={"tp": dev}, device_id_type=MESH
        )

    def place(c, h, piece):
        return pl.ds(pl.multiple_of(c * m + h * half + piece * q, q), q)

    def piece(p):
        return pl.ds(pl.multiple_of(p * q, q), q)

    def cols(p, width):
        return pl.ds(pl.multiple_of(p * width, width), width)

    lo, hi, al = pl.ds(0, ch), pl.ds(ch, ch), pl.ds(0, d)

    def same(c, k, r, w, dev):
        return send(c, k, dx.at[r, w], dx.at[r, w], dev)

    def copy(c, k):
        if k == 0:
            return send(c, 0, sT.at[c], rT.at[c], partner)
        if k <= 2:
            return send(c, k, sA.at[c, k - 1], rA.at[c, k - 1], first[k - 1])
        if k <= 4:
            return send(c, k, sB.at[c, k - 3], rB.at[c, k - 3], first[k - 3])
        if k <= 6:
            return send(c, k, sC.at[c, k - 5], rC.at[c, k - 5], second[k - 5])
        if k <= 8:
            return send(c, k, sD.at[c, k - 7], rD.at[c, k - 7], second[k - 7])
        mine = place(c, core, p1)
        if k <= 10:
            return same(c, k, mine, cols(p2, cq), second[k - 9])
        if k == 11:
            return same(c, k, mine, cols(2 * l2, ce), second[0])
        if k == 12:
            return same(c, k, mine, cols(2 * r2 + 1, ce), second[1])
        if k <= 14:
            return same(c, k, mine, al, first[k - 13])
        if k == 15:
            return same(c, k, place(c, core, l1), lo, first[0])
        if k == 16:
            return same(c, k, place(c, core, r1), hi, first[1])
        return same(c, k, place(c, core, (p1, l1, r1, o1)[k - 17]), al, partner)

    def arrival(c, k):
        if k <= 8:
            return copy(c, k)
        mine = place(c, core, p1)
        if k <= 10:
            return same(c, k, mine, cols((l2, r2)[k - 9], cq), partner)
        if k <= 12:
            return same(c, k, mine, cols(2 * o2 + (k - 11), ce), partner)
        if k <= 14:
            return same(c, k, place(c, core, (l1, r1)[k - 13]), al, partner)
        if k <= 16:
            return same(c, k, place(c, core, o1), (lo, hi)[k - 15], partner)
        s = (p2, l2, r2, o2)[k - 17]
        return same(c, k, place(c, 1 - core, s), al, partner)

    def got(c, *ks):
        for k in ks:
            arrival(c, k).wait_recv()

    def go(c, *ks):
        for k in ks:
            copy(c, k).start()

    def event(k, c):
        acc = own.at[lax.rem(c, SLOTS)]
        if k == 1:
            got(c, 0)
            t = acc[piece(o1), :] + rT[c, piece(o1), :].astype(F32)
            sA[c, 0] = t[:, :ch].astype(BF16)
            sA[c, 1] = t[:, ch:].astype(BF16)
            for p in (r1, l1, p1):
                acc[piece(p), :] = acc[piece(p), :] + rT[c, piece(p), :].astype(F32)
            go(c, 1, 2)
        elif k == 2:
            got(c, 1, 2)
            sB[c, 0, :, lo] = (acc[piece(r1), lo] + rA[c, 0].astype(F32)).astype(BF16)
            sB[c, 0, :, hi] = acc[piece(r1), hi].astype(BF16)
            sB[c, 1, :, lo] = acc[piece(l1), lo].astype(BF16)
            sB[c, 1, :, hi] = (acc[piece(l1), hi] + rA[c, 1].astype(F32)).astype(BF16)
            go(c, 3, 4)
        elif k == 3:
            got(c, 3, 4)
            acc[piece(p1), :] = acc[piece(p1), :] + rB[c, 0].astype(F32) + rB[c, 1].astype(F32)
            sC[c, 0] = acc[piece(p1), cols(2 * o2, ce)].astype(BF16)
            sC[c, 1] = acc[piece(p1), cols(2 * o2 + 1, ce)].astype(BF16)
            go(c, 5, 6)
        elif k == 4:
            got(c, 5, 6)
            sD[c, 0, :, :ce] = (acc[piece(p1), cols(2 * r2, ce)] + rC[c, 0].astype(F32)).astype(BF16)
            sD[c, 0, :, ce:] = acc[piece(p1), cols(2 * r2 + 1, ce)].astype(BF16)
            sD[c, 1, :, :ce] = acc[piece(p1), cols(2 * l2, ce)].astype(BF16)
            sD[c, 1, :, ce:] = (acc[piece(p1), cols(2 * l2 + 1, ce)] + rC[c, 1].astype(F32)).astype(BF16)
            go(c, 7, 8)
        elif k == 5:
            got(c, 7, 8)
            t = acc[piece(p1), cols(p2, cq)] + rD[c, 0].astype(F32) + rD[c, 1].astype(F32)
            dx[place(c, core, p1), cols(p2, cq)] = t.astype(BF16)
            go(c, 9, 10)
        elif k == 6:
            got(c, 9, 10)
            go(c, 11, 12)
        elif k == 7:
            got(c, 11, 12)
            go(c, 13, 14, 17)
        elif k == 8:
            got(c, 13, 14)
            go(c, 15, 16, 18, 19)
        elif k == 9:
            got(c, 15, 16)
            go(c, 20)
        else:
            got(c, 17, 18, 19, 20)

    c0, c1 = math.sqrt(2 / math.pi), math.sqrt(2 / math.pi) * 0.044715

    def hidden_part(c):
        for cp in chunk_loads(c):
            cp.wait()
        r = pl.ds(pl.multiple_of(c * m, m), m)
        for lo_f in range(0, f, f // 2):
            w = pl.ds(lo_f, f // 2)
            w2 = pl.ds(f + lo_f, f // 2)
            dh = dot(dyv[r, :], wdv[w, :], 1, 1)
            g = gu[r, w].astype(F32)
            u = gu[r, w2].astype(F32)
            g2 = g * g
            t = jnp.tanh(g * (c0 + c1 * g2))
            hg = 0.5 * g
            s = 1.0 + t
            act = hg * s
            slope = 0.5 * s + hg * (s * (1.0 - t)) * (c0 + (3.0 * c1) * g2)
            hid[r, w] = (act * u).astype(BF16)
            gu[r, w] = (dh * u * slope).astype(BF16)
            gu[r, w2] = (dh * act).astype(BF16)

    def term_part(c):
        base = c * m
        rp = pl.ds(pl.multiple_of(base + (1 - core) * half, half), half)
        ro = pl.ds(pl.multiple_of(base + core * half, half), half)
        acc = own.at[lax.rem(c, SLOTS)]
        lhs = jnp.concatenate([gu[rp, :], gu[ro, :]], 0)
        for k in range(4):
            w = pl.ds(k * cq, cq)
            t = dot(lhs, wv[w, :], 1, 1)
            sT[c, :, w] = t[:half].astype(BF16)
            acc[:, w] = t[half:]
        go(c, 0)

    def weights_part(j):
        unit_load(j, lax.rem(j, 2)).wait()
        r = pl.ds(pl.multiple_of(j * uw, uw), uw)
        t = dot(xs[lax.rem(j, 2)], gu[...], 0, 0)
        dwg[r, :] = t[:, :f].astype(BF16)
        dwu[r, :] = t[:, f:].astype(BF16)

    def down_part(j):
        w = pl.ds(pl.multiple_of(j * uw, uw), uw)
        dwd[:, w] = dot(hid[...], dyv[:, w], 0, 0).astype(BF16)

    load_wd.wait()

    def step(t, _):
        @pl.when(t < n)
        def _():
            hidden_part(t)

        j = t - n

        @pl.when((j >= 0) & (j < units))
        def _():
            weights_part(j)

            @pl.when(j + 2 < units)
            def _():
                unit_load(j + 2, lax.rem(j, 2)).start()

        for k in range(1, 11):
            @pl.when((t - k >= 0) & (t - k < n))
            def _(k=k):
                event(k, t - k)

        @pl.when(t == 0)
        def _():
            load_wg.wait()
            load_wu.wait()

        @pl.when(t < n)
        def _():
            term_part(t)

            @pl.when(t + 3 < n)
            def _():
                for cp in chunk_loads(t + 3):
                    cp.start()

        @pl.when(t == n - 3)
        def _():
            unit_load(0, 0).start()
            unit_load(1, 1).start()

        @pl.when((j >= 0) & (j < units))
        def _():
            down_part(j)

        return 0

    lax.fori_loop(0, n + 10, step, 0)

    def drain(c, _):
        for k in range(COPIES):
            copy(c, k).wait_send()
        return 0

    lax.fori_loop(0, n, drain, 0)


def solution(mesh):
    side = math.isqrt(mesh.shape["tp"] // 2)

    def step(x, dy, gate, up, w_gate, w_up, w_down):
        (rows, d), f = x.shape, gate.shape[1]
        m = min(CHUNK, rows)
        n, half, q = rows // m, m // 2, m // 8
        vm = pltpu.VMEM
        return tuple(pl.pallas_call(
            functools.partial(kernel, side),
            out_shape=[vm((rows, d), BF16), vm((d, f), BF16), vm((d, f), BF16), vm((f, d), BF16)],
            in_specs=[pl.BlockSpec(memory_space=pl.ANY)] * 7,
            out_specs=[pl.BlockSpec(memory_space=pltpu.VMEM)] * 4,
            scratch_shapes=[
                vm((f, d), BF16), vm((d, 2 * f), BF16), vm((rows, d), BF16), vm((rows, 2 * f), BF16), vm((rows, f), BF16),
                vm((2, rows, d // n), BF16), vm((SLOTS, half, d), F32),
                vm((n, half, d), BF16), vm((n, half, d), BF16),
                vm((n, 2, q, d // 2), BF16), vm((n, 2, q, d // 2), BF16),
                vm((n, 2, q, d), BF16), vm((n, 2, q, d), BF16),
                vm((n, 2, q, d // 8), BF16), vm((n, 2, q, d // 8), BF16),
                vm((n, 2, q, d // 4), BF16), vm((n, 2, q, d // 4), BF16),
                pltpu.SemaphoreType.DMA((3,)), pltpu.SemaphoreType.DMA((n, 3)), pltpu.SemaphoreType.DMA((2,)),
                pltpu.SemaphoreType.DMA((n, COPIES)), pltpu.SemaphoreType.DMA((n, COPIES)),
            ],
            compiler_params=pltpu.CompilerParams(
                collective_id=0, has_side_effects=True, vmem_limit_bytes=49 * 2**20
            ),
        )(x, dy, gate, up, w_gate, w_up, w_down))

    tokens, columns, by_rows = P("dp", None), P(None, "tp"), P("tp", None)
    return jax.shard_map(
        step,
        mesh=mesh,
        in_specs=(tokens, tokens, P("dp", "tp"), P("dp", "tp"), columns, columns, by_rows),
        out_specs=(tokens, P("dp", "tp"), P("dp", "tp"), P(("dp", "tp"), None)),
        check_vma=False,
    )
```

time: 176 us -> 91.1 us (0.52)
  Pallas kernels: 0 us -> 83 us
  waiting for transfers between devices: 77.9 us -> 0 us
  matrix products: 70.6 us -> 0 us
  between operations: 14.1 us -> 0.64 us
  local copies, waits for them, and re-layouts: 13.6 us -> 7.35 us
    pallas_call x0 -> x1, Pallas kernels: none -> 83 us  [step(): pl.pallas_call(functools.partial(kernel, side), out_shape=[vm((rows, d),...]
    psum x1 -> x0, waiting for transfers between devices: 77.8 us -> none  [step(): dx = lax.psum(term.astype(jnp.bfloat16), 'tp')]
    dot_general x6 -> x0, matrix products: 70.6 us -> none  [the longest x1 16.9 us: step(): jnp.dot(d_up, w_up.T, preferred_element_type=jnp.float32)]
    unnamed x9 -> x4, local copies, waits for them, and re-layouts: 13.6 us -> 7.35 us
  transfers between devices with their start and end apart: 1 -> 0, of which waited for: 1 -> 0; matrix products, arithmetic and copies ran while one was open for 20% -> 0% of each run, Pallas kernels for 0% -> 0%
where the time goes in v1:
time: 91.1 us; the launch traced here: 91 us
  Pallas kernels  83 us (91%)
  local copies, waits for them, and re-layouts  7.35 us (8%)
    pallas_call x1, Pallas kernels, step(): pl.pallas_call(functools.partial(kernel, side), out_shape=[vm((rows, d),...  83 us
    unnamed x4, local copies, waits for them, and re-layouts  7.35 us

profile of v1, /device:TPU:97, one launch (start us, length us, event | category | flops | bytes accessed | tf_op | source)
XLA Modules:
  0.0 91.0 jit_solution(1919713307729466505)
XLA Ops:
  0.6 83.0 %shard_map.102 = (bf16[2048,2048]{1,0:T(8,128)(2,1)S(1)}, bf16[2048,512]{1,0:T(8,128)(2,1)S(1)}, bf16[2048,512]{1,0:T(8,128)(2,1)S(1)}, bf16[512,2048]{1,0:T(8,128)(2,1)S(1)}) custom-call(bf16[2048,2048]{1,0:T(8,128)(2,1)} %x.1, bf16[2048,2048]{1,0:T(8,128)(2,1)} %dy.1, bf16[2048,512]{1,0:T(8,128)(2,1)} %gate.1, bf16[2048,512]{1,0:T(8,128)(2,1)} %up.1, ...), custom_call_target="tpu_custom_call" | custom-call | tf_op jit(solution)/shard_map/pallas_call | solution.py:311
  83.7 3.4 %copy.15 = bf16[2048,2048]{1,0:T(8,128)(2,1)} copy(bf16[2048,2048]{1,0:T(8,128)(2,1)S(1)} %get-tuple-element.4) | data formatting | bytes 16777216
  87.1 1.3 %copy.16 = bf16[2048,512]{1,0:T(8,128)(2,1)} copy(bf16[2048,512]{1,0:T(8,128)(2,1)S(1)} %get-tuple-element.5) | data formatting | bytes 4194304
  88.4 1.3 %copy.17 = bf16[2048,512]{1,0:T(8,128)(2,1)} copy(bf16[2048,512]{1,0:T(8,128)(2,1)S(1)} %get-tuple-element.6) | data formatting | bytes 4194304
  89.7 1.3 %copy.18 = bf16[512,2048]{1,0:T(8,128)(2,1)} copy(bf16[512,2048]{1,0:T(8,128)(2,1)S(1)} %get-tuple-element.7) | data formatting | bytes 4194304

commit v2 on v1

v2 whole, which is shorter than its diff:
```python
import functools
import math

import jax
import jax.numpy as jnp
from jax import lax
from jax.experimental import pallas as pl
from jax.experimental.pallas import tpu as pltpu
from jax.sharding import PartitionSpec as P

MESH = pl.DeviceIdType.MESH
CHUNK = 256
BF16, F32 = jnp.bfloat16, jnp.float32
COPIES = 19
SLOTS = 6
POINTS = 3
LAG = {1: 4, 2: 9, 3: 14, 4: 20, 5: 28, 6: 43, 7: 75, 8: 81}


def dot(a, b, ca, cb):
    return lax.dot_general(a, b, (((ca,), (cb,)), ((), ())), preferred_element_type=F32)


def kernel(side, x, dy, gate, up, wg, wu, wd, dx, dwg, dwu, dwd,
           wdv, wv, dyv, gu, hid, xs, own, fin, sT, rT, sA, rA, sB, rB, sC, rC, wsem, lsem, xsem, ssem, rsem):
    rows, d = dx.shape
    f = wd.shape[0]
    m = min(CHUNK, rows)
    n = rows // m
    half, q = m // 2, m // 8
    ch, cq = d // 2, d // 4
    units, uw = n, d // n

    me = lax.axis_index("tp")
    core = lax.rem(me, 2)
    chip = me // 2
    px, py = chip // side, lax.rem(chip, side)
    p1 = px + core * (py - px)
    p2 = py + core * (px - py)

    def at(a, b):
        return ((1 - core) * (a * side + b) + core * (b * side + a)) * 2 + core

    def turn(p, k):
        return lax.rem(p + k, side)

    r1, o1, l1 = turn(p1, 1), turn(p1, 2), turn(p1, 3)
    r2, o2, l2 = turn(p2, 1), turn(p2, 2), turn(p2, 3)
    partner = me + 1 - 2 * core
    first = (at(r1, p2), at(l1, p2))
    second = (at(p1, r2), at(p1, l2), at(p1, o2))

    barrier = pltpu.get_barrier_semaphore()
    for dev in (partner, *first, *second):
        pl.semaphore_signal(barrier, inc=1, device_id={"tp": dev}, device_id_type=MESH)

    def load(src, dst, sem):
        return pltpu.make_async_copy(src, dst, sem)

    def chunk_loads(c):
        r = pl.ds(pl.multiple_of(c * m, m), m)
        return (
            load(dy.at[r], dyv.at[r], lsem.at[c, 0]),
            load(gate.at[r], gu.at[r, pl.ds(0, f)], lsem.at[c, 1]),
            load(up.at[r], gu.at[r, pl.ds(f, f)], lsem.at[c, 2]),
        )

    def unit_load(j, slot):
        return load(x.at[:, pl.ds(pl.multiple_of(j * uw, uw), uw)], xs.at[slot], xsem.at[slot])

    load_wd = load(wd, wdv, wsem.at[0])
    load_wg = load(wg, wv.at[:, pl.ds(0, f)], wsem.at[1])
    load_wu = load(wu, wv.at[:, pl.ds(f, f)], wsem.at[2])
    first_loads = chunk_loads(0)
    for cp in (first_loads[1], first_loads[2], first_loads[0], load_wd):
        cp.start()

    def send(c, k, src, dst, dev):
        return pltpu.make_async_remote_copy(
            src, dst, ssem.at[c, k], rsem.at[c, k], device_id={"tp": dev}, device_id_type=MESH
        )

    def place(c, h, piece):
        return pl.ds(pl.multiple_of(c * m + h * half + piece * q, q), q)

    def piece(p):
        return pl.ds(pl.multiple_of(p * q, q), q)

    def cols(p, width):
        return pl.ds(pl.multiple_of(p * width, width), width)

    lo, hi, al = pl.ds(0, ch), pl.ds(ch, ch), pl.ds(0, d)

    def same(c, k, r, w, dev):
        return send(c, k, dx.at[r, w], dx.at[r, w], dev)

    def copy(c, k):
        if k == 0:
            return send(c, 0, sT.at[c], rT.at[c], partner)
        if k <= 2:
            return send(c, k, sA.at[c, k - 1], rA.at[c, k - 1], first[k - 1])
        if k <= 4:
            return send(c, k, sB.at[c, k - 3], rB.at[c, k - 3], first[k - 3])
        if k <= 7:
            return send(c, k, sC.at[c, k - 5], rC.at[c, k - 5], second[k - 5])
        mine = place(c, core, p1)
        if k <= 10:
            return same(c, k, mine, cols(p2, cq), second[k - 8])
        if k <= 12:
            return same(c, k, mine, al, first[k - 11])
        if k == 13:
            return same(c, k, place(c, core, l1), lo, first[0])
        if k == 14:
            return same(c, k, place(c, core, r1), hi, first[1])
        return same(c, k, place(c, core, (p1, l1, r1, o1)[k - 15]), al, partner)

    def arrival(c, k):
        if k <= 7:
            return copy(c, k)
        mine = place(c, core, p1)
        if k <= 10:
            return same(c, k, mine, cols((l2, r2, o2)[k - 8], cq), partner)
        if k <= 12:
            return same(c, k, place(c, core, (l1, r1)[k - 11]), al, partner)
        if k <= 14:
            return same(c, k, place(c, core, o1), (lo, hi)[k - 13], partner)
        s = (p2, l2, r2, o2)[k - 15]
        return same(c, k, place(c, 1 - core, s), al, partner)

    def got(c, *ks):
        for k in ks:
            arrival(c, k).wait_recv()

    def go(c, *ks):
        for k in ks:
            copy(c, k).start()

    def event(k, c):
        acc = own.at[lax.rem(c, SLOTS)]
        if k == 1:
            got(c, 0)
            t = acc[piece(o1), :] + rT[c, piece(o1), :].astype(F32)
            sA[c, 0] = t[:, :ch].astype(BF16)
            sA[c, 1] = t[:, ch:].astype(BF16)
            for p in (r1, l1, p1):
                acc[piece(p), :] = acc[piece(p), :] + rT[c, piece(p), :].astype(F32)
            go(c, 1, 2)
        elif k == 2:
            got(c, 1, 2)
            sB[c, 0, :, lo] = (acc[piece(r1), lo] + rA[c, 0].astype(F32)).astype(BF16)
            sB[c, 0, :, hi] = acc[piece(r1), hi].astype(BF16)
            sB[c, 1, :, lo] = acc[piece(l1), lo].astype(BF16)
            sB[c, 1, :, hi] = (acc[piece(l1), hi] + rA[c, 1].astype(F32)).astype(BF16)
            go(c, 3, 4)
        elif k == 3:
            got(c, 3, 4)
            acc[piece(p1), :] = acc[piece(p1), :] + rB[c, 0].astype(F32) + rB[c, 1].astype(F32)
            for i, p in enumerate((r2, l2, o2)):
                sC[c, i] = acc[piece(p1), cols(p, cq)].astype(BF16)
            fin[c] = acc[piece(p1), cols(p2, cq)]
            go(c, 5, 6, 7)
        elif k == 4:
            got(c, 5, 6, 7)
            t = fin[c] + rC[c, 0].astype(F32) + rC[c, 1].astype(F32) + rC[c, 2].astype(F32)
            dx[place(c, core, p1), cols(p2, cq)] = t.astype(BF16)
            go(c, 8, 9, 10)
        elif k == 5:
            got(c, 8, 9, 10)
            go(c, 11, 12, 15)
        elif k == 6:
            got(c, 11, 12)
            go(c, 13, 14, 16, 17)
        elif k == 7:
            got(c, 13, 14)
            go(c, 18)
        else:
            got(c, 15, 16, 17, 18)

    c0, c1 = math.sqrt(2 / math.pi), math.sqrt(2 / math.pi) * 0.044715

    def hidden_part(c):
        r = pl.ds(pl.multiple_of(c * m, m), m)
        w, w2 = pl.ds(0, f), pl.ds(f, f)
        dh = dot(dyv[r, :], wdv[w, :], 1, 1)
        g = gu[r, w].astype(F32)
        u = gu[r, w2].astype(F32)
        g2 = g * g
        t = jnp.tanh(g * (c0 + c1 * g2))
        hg = 0.5 * g
        s = 1.0 + t
        act = hg * s
        slope = 0.5 * s + hg * (s * (1.0 - t)) * (c0 + (3.0 * c1) * g2)
        hid[r, w] = (act * u).astype(BF16)
        gu[r, w] = (dh * u * slope).astype(BF16)
        gu[r, w2] = (dh * act).astype(BF16)

    def term_part(c, k):
        base = c * m
        rp = pl.ds(pl.multiple_of(base + (1 - core) * half, half), half)
        ro = pl.ds(pl.multiple_of(base + core * half, half), half)
        w = pl.ds(k * ch, ch)
        t = dot(jnp.concatenate([gu[rp, :], gu[ro, :]], 0), wv[w, :], 1, 1)
        sT[c, :, w] = t[:half].astype(BF16)
        own[lax.rem(c, SLOTS), :, w] = t[half:]

    def weights_part(j):
        r = pl.ds(pl.multiple_of(j * uw, uw), uw)
        t = dot(xs[lax.rem(j, 2)], gu[...], 0, 0)
        dwg[r, :] = t[:, :f].astype(BF16)
        dwu[r, :] = t[:, f:].astype(BF16)

    def down_part(j):
        w = pl.ds(pl.multiple_of(j * uw, uw), uw)
        dwd[:, w] = dot(hid[...], dyv[:, w], 0, 0).astype(BF16)

    def dx_piece(c, i):
        if i == 0:
            for cp in chunk_loads(c):
                cp.wait()
            hidden_part(c)
        else:
            term_part(c, i - 1)
        if i == 2:
            go(c, 0)

            @pl.when(c + 3 < n)
            def _():
                for cp in chunk_loads(c + 3):
                    cp.start()

            @pl.when(c == n - 3)
            def _():
                unit_load(0, 0).start()
                unit_load(1, 1).start()

    def dw_piece(j, i):
        if i == 0:
            unit_load(j, lax.rem(j, 2)).wait()
            weights_part(j)

            @pl.when(j + 2 < units)
            def _():
                unit_load(j + 2, lax.rem(j, 2)).start()
        elif i == 2:
            down_part(j)

    first_loads[1].wait()
    load_wg.start()
    load_wu.start()
    first_loads[2].wait()
    first_loads[0].wait()
    load_wd.wait()
    hidden_part(0)
    for c in range(1, min(4, n)):
        for cp in chunk_loads(c):
            cp.start()
    load_wg.wait()
    load_wu.wait()
    term_part(0, 0)
    term_part(0, 1)
    pl.semaphore_wait(barrier, 6)
    go(0, 0)

    def step(t, _):
        for i in range(POINTS):
            @pl.when(t < n)
            def _(i=i):
                dx_piece(t, i)

            if i != 1:
                @pl.when((t >= n) & (t < n + units))
                def _(i=i):
                    dw_piece(t - n, i)

            for k, lag in LAG.items():
                if lag % POINTS == i:
                    c = t - lag // POINTS

                    @pl.when((c >= 0) & (c < n))
                    def _(k=k, c=c):
                        event(k, c)

        return 0

    lax.fori_loop(1, n + max(LAG.values()) // POINTS, step, 0)

    def drain(c, _):
        for k in range(COPIES):
            copy(c, k).wait_send()
        return 0

    lax.fori_loop(0, n, drain, 0)


def flush(*refs):
    src, dst, sem = refs[:4], refs[4:8], refs[8]
    copies, cuts = [], (8, 2, 2, 2)
    for a, b, cut in zip(src, dst, cuts):
        size = a.shape[0] // cut
        for i in range(cut):
            r = pl.ds(i * size, size)
            copies.append(pltpu.make_async_copy(a.at[r], b.at[r], sem.at[len(copies)]))
    for cp in copies:
        cp.start()
    for cp in copies:
        cp.wait()


def solution(mesh):
    side = math.isqrt(mesh.shape["tp"] // 2)

    def step(x, dy, gate, up, w_gate, w_up, w_down):
        (rows, d), f = x.shape, gate.shape[1]
        m = min(CHUNK, rows)
        n, half, q = rows // m, m // 2, m // 8
        vm = pltpu.VMEM
        results = pl.pallas_call(
            functools.partial(kernel, side),
            out_shape=[vm((rows, d), BF16), vm((d, f), BF16), vm((d, f), BF16), vm((f, d), BF16)],
            in_specs=[pl.BlockSpec(memory_space=pl.ANY)] * 7,
            out_specs=[pl.BlockSpec(memory_space=pltpu.VMEM)] * 4,
            scratch_shapes=[
                vm((f, d), BF16), vm((d, 2 * f), BF16), vm((rows, d), BF16), vm((rows, 2 * f), BF16), vm((rows, f), BF16),
                vm((2, rows, d // n), BF16), vm((SLOTS, half, d), F32), vm((n, q, d // 4), F32),
                vm((n, half, d), BF16), vm((n, half, d), BF16),
                vm((n, 2, q, d // 2), BF16), vm((n, 2, q, d // 2), BF16),
                vm((n, 2, q, d), BF16), vm((n, 2, q, d), BF16),
                vm((n, 3, q, d // 4), BF16), vm((n, 3, q, d // 4), BF16),
                pltpu.SemaphoreType.DMA((3,)), pltpu.SemaphoreType.DMA((n, 3)), pltpu.SemaphoreType.DMA((2,)),
                pltpu.SemaphoreType.DMA((n, COPIES)), pltpu.SemaphoreType.DMA((n, COPIES)),
            ],
            compiler_params=pltpu.CompilerParams(
                collective_id=0, has_side_effects=True, vmem_limit_bytes=49 * 2**20 + 2**19
            ),
        )(x, dy, gate, up, w_gate, w_up, w_down)
        return tuple(pl.pallas_call(
            flush,
            out_shape=[jax.ShapeDtypeStruct(a.shape, a.dtype) for a in results],
            in_specs=[pl.BlockSpec(memory_space=pltpu.VMEM)] * 4,
            out_specs=[pl.BlockSpec(memory_space=pl.ANY)] * 4,
            scratch_shapes=[pltpu.SemaphoreType.DMA((14,))],
            compiler_params=pltpu.CompilerParams(vmem_limit_bytes=2**20),
        )(*results))

    tokens, columns, by_rows = P("dp", None), P(None, "tp"), P("tp", None)
    return jax.shard_map(
        step,
        mesh=mesh,
        in_specs=(tokens, tokens, P("dp", "tp"), P("dp", "tp"), columns, columns, by_rows),
        out_specs=(tokens, P("dp", "tp"), P("dp", "tp"), P(("dp", "tp"), None)),
        check_vma=False,
    )
```

time: 91.1 us -> 76.5 us (0.84)
  local copies, waits for them, and re-layouts: 7.35 us -> 0 us
  Pallas kernels: 83 us -> 75.7 us
    pallas_call x1, Pallas kernels: 83 us -> 70.4 us  [step(): pl.pallas_call(functools.partial(kernel, side), out_shape=[vm((rows, d),...]
    unnamed x4 -> x0, local copies, waits for them, and re-layouts: 7.35 us -> none
    pallas_call x0 -> x1, Pallas kernels: none -> 5.32 us  [step(): pl.pallas_call(flush, out_shape=[jax.ShapeDtypeStruct(a.shape, a.dtype) f...]
where the time goes in v2:
time: 76.5 us; the launch traced here: 76.4 us
  Pallas kernels  75.7 us (99%)
    pallas_call x1, Pallas kernels, step(): pl.pallas_call(functools.partial(kernel, side), out_shape=[vm((rows, d),...  70.4 us
    pallas_call x1, Pallas kernels, step(): pl.pallas_call(flush, out_shape=[jax.ShapeDtypeStruct(a.shape, a.dtype) f...  5.32 us

profile of v2, /device:TPU:97, one launch (start us, length us, event | category | flops | bytes accessed | tf_op | source)
XLA Modules:
  0.0 76.4 jit_solution(1372418247289951581)
XLA Ops:
  0.6 70.4 %shard_map.102 = (bf16[2048,2048]{1,0:T(8,128)(2,1)S(1)}, bf16[2048,512]{1,0:T(8,128)(2,1)S(1)}, bf16[2048,512]{1,0:T(8,128)(2,1)S(1)}, bf16[512,2048]{1,0:T(8,128)(2,1)S(1)}) custom-call(bf16[2048,2048]{1,0:T(8,128)(2,1)} %x.1, bf16[2048,2048]{1,0:T(8,128)(2,1)} %dy.1, bf16[2048,512]{1,0:T(8,128)(2,1)} %gate.1, bf16[2048,512]{1,0:T(8,128)(2,1)} %up.1, ...), custom_call_target="tpu_custom_call" | custom-call | tf_op jit(solution)/shard_map/pallas_call | solution.py:317
  71.1 5.3 %shard_map.103 = (bf16[2048,2048]{1,0:T(8,128)(2,1)}, bf16[2048,512]{1,0:T(8,128)(2,1)}, bf16[2048,512]{1,0:T(8,128)(2,1)}, bf16[512,2048]{1,0:T(8,128)(2,1)}) custom-call(bf16[2048,2048]{1,0:T(8,128)(2,1)S(1)} %get-tuple-element.8.refs_0_, bf16[2048,512]{1,0:T(8,128)(2,1)S(1)} %get-tuple-element.9.refs_1_, bf16[2048,512]{1,0:T(8,128)(2,1)S(1)} %get-tuple-element.10.refs_2_, ...), custom_call_target="tpu_custom_call" | custom-call | tf_op jit(solution)/shard_map/pallas_call | solution.py:336

commit v3 on v2

--- a/solution.py
+++ b/solution.py
@@ -13,8 +13,8 @@
 BF16, F32 = jnp.bfloat16, jnp.float32
 COPIES = 19
 SLOTS = 6
-POINTS = 3
-LAG = {1: 4, 2: 9, 3: 14, 4: 20, 5: 28, 6: 43, 7: 75, 8: 81}
+POINTS = 2
+LAG = {1: 3, 2: 7, 3: 12, 4: 17, 5: 22, 6: 35, 7: 52, 8: 58}
 
 
 def dot(a, b, ca, cb):
@@ -77,7 +77,7 @@
 
     def send(c, k, src, dst, dev):
         return pltpu.make_async_remote_copy(
-            src, dst, ssem.at[c, k], rsem.at[c, k], device_id={"tp": dev}, device_id_type=MESH
+            src, dst, ssem.at[c], rsem.at[c, k], device_id={"tp": dev}, device_id_type=MESH
         )
 
     def place(c, h, piece):
@@ -194,14 +194,16 @@
         gu[r, w] = (dh * u * slope).astype(BF16)
         gu[r, w2] = (dh * act).astype(BF16)
 
-    def term_part(c, k):
+    def term_part(c):
         base = c * m
         rp = pl.ds(pl.multiple_of(base + (1 - core) * half, half), half)
         ro = pl.ds(pl.multiple_of(base + core * half, half), half)
-        w = pl.ds(k * ch, ch)
-        t = dot(jnp.concatenate([gu[rp, :], gu[ro, :]], 0), wv[w, :], 1, 1)
-        sT[c, :, w] = t[:half].astype(BF16)
-        own[lax.rem(c, SLOTS), :, w] = t[half:]
+        lhs = jnp.concatenate([gu[rp, :], gu[ro, :]], 0)
+        for k in range(4):
+            w = pl.ds(k * cq, cq)
+            t = dot(lhs, wv[w, :], 1, 1)
+            sT[c, :, w] = t[:half].astype(BF16)
+            own[lax.rem(c, SLOTS), :, w] = t[half:]
 
     def weights_part(j):
         r = pl.ds(pl.multiple_of(j * uw, uw), uw)
@@ -219,8 +221,7 @@
                 cp.wait()
             hidden_part(c)
         else:
-            term_part(c, i - 1)
-        if i == 2:
+            term_part(c)
             go(c, 0)
 
             @pl.when(c + 3 < n)
@@ -241,7 +242,7 @@
             @pl.when(j + 2 < units)
             def _():
                 unit_load(j + 2, lax.rem(j, 2)).start()
-        elif i == 2:
+        else:
             down_part(j)
 
     first_loads[1].wait()
@@ -256,8 +257,7 @@
             cp.start()
     load_wg.wait()
     load_wu.wait()
-    term_part(0, 0)
-    term_part(0, 1)
+    term_part(0)
     pl.semaphore_wait(barrier, 6)
     go(0, 0)
 
@@ -267,10 +267,9 @@
             def _(i=i):
                 dx_piece(t, i)
 
-            if i != 1:
-                @pl.when((t >= n) & (t < n + units))
-                def _(i=i):
-                    dw_piece(t - n, i)
+            @pl.when((t >= n) & (t < n + units))
+            def _(i=i):
+                dw_piece(t - n, i)
 
             for k, lag in LAG.items():
                 if lag % POINTS == i:
@@ -284,12 +283,9 @@
 
     lax.fori_loop(1, n + max(LAG.values()) // POINTS, step, 0)
 
-    def drain(c, _):
-        for k in range(COPIES):
-            copy(c, k).wait_send()
-        return 0
-
-    lax.fori_loop(0, n, drain, 0)
+    sent = pl.ds(0, half + (2 + 1) * q + 2 * 3 * q // 4 + (2 + 1) * q + 4 * q)
+    for c in range(n):
+        pltpu.make_async_copy(dx.at[sent], dx.at[sent], ssem.at[c]).wait()
 
 
 def flush(*refs):
@@ -327,7 +323,7 @@
                 vm((n, 2, q, d), BF16), vm((n, 2, q, d), BF16),
                 vm((n, 3, q, d // 4), BF16), vm((n, 3, q, d // 4), BF16),
                 pltpu.SemaphoreType.DMA((3,)), pltpu.SemaphoreType.DMA((n, 3)), pltpu.SemaphoreType.DMA((2,)),
-                pltpu.SemaphoreType.DMA((n, COPIES)), pltpu.SemaphoreType.DMA((n, COPIES)),
+                pltpu.SemaphoreType.DMA((n,)), pltpu.SemaphoreType.DMA((n, COPIES)),
             ],
             compiler_params=pltpu.CompilerParams(
                 collective_id=0, has_side_effects=True, vmem_limit_bytes=49 * 2**20 + 2**19

time: 76.5 us -> 73.6 us (0.962)
  Pallas kernels: 75.7 us -> 72.8 us
    pallas_call x1, Pallas kernels: 70.4 us -> 67.5 us  [step(): pl.pallas_call(functools.partial(kernel, side), out_shape=[vm((rows, d),...]
where the time goes in v3:
time: 73.6 us; the launch traced here: 73.5 us
  Pallas kernels  72.8 us (99%)
    pallas_call x1, Pallas kernels, step(): pl.pallas_call(functools.partial(kernel, side), out_shape=[vm((rows, d),...  67.5 us
    pallas_call x1, Pallas kernels, step(): pl.pallas_call(flush, out_shape=[jax.ShapeDtypeStruct(a.shape, a.dtype) f...  5.32 us

profile of v3, /device:TPU:97, one launch (start us, length us, event | category | flops | bytes accessed | tf_op | source)
XLA Modules:
  0.0 73.5 jit_solution(15569432226789686743)
XLA Ops:
  0.6 67.5 %shard_map.102 = (bf16[2048,2048]{1,0:T(8,128)(2,1)S(1)}, bf16[2048,512]{1,0:T(8,128)(2,1)S(1)}, bf16[2048,512]{1,0:T(8,128)(2,1)S(1)}, bf16[512,2048]{1,0:T(8,128)(2,1)S(1)}) custom-call(bf16[2048,2048]{1,0:T(8,128)(2,1)} %x.1, bf16[2048,2048]{1,0:T(8,128)(2,1)} %dy.1, bf16[2048,512]{1,0:T(8,128)(2,1)} %gate.1, bf16[2048,512]{1,0:T(8,128)(2,1)} %up.1, ...), custom_call_target="tpu_custom_call" | custom-call | tf_op jit(solution)/shard_map/pallas_call | solution.py:313
  68.2 5.3 %shard_map.103 = (bf16[2048,2048]{1,0:T(8,128)(2,1)}, bf16[2048,512]{1,0:T(8,128)(2,1)}, bf16[2048,512]{1,0:T(8,128)(2,1)}, bf16[512,2048]{1,0:T(8,128)(2,1)}) custom-call(bf16[2048,2048]{1,0:T(8,128)(2,1)S(1)} %get-tuple-element.8.refs_0_, bf16[2048,512]{1,0:T(8,128)(2,1)S(1)} %get-tuple-element.9.refs_1_, bf16[2048,512]{1,0:T(8,128)(2,1)S(1)} %get-tuple-element.10.refs_2_, ...), custom_call_target="tpu_custom_call" | custom-call | tf_op jit(solution)/shard_map/pallas_call | solution.py:332

commit v4 on v3

--- a/solution.py
+++ b/solution.py
@@ -10,11 +10,12 @@
 
 MESH = pl.DeviceIdType.MESH
 CHUNK = 256
+PARTS = 2
 BF16, F32 = jnp.bfloat16, jnp.float32
-COPIES = 19
-SLOTS = 6
+EVENT = (0, 1, 1, 2, 2, 3, 3, 3, 4, 4, 4, 5, 5, 6, 6, 7, 7, 7, 7)
+SLOTS = 12
 POINTS = 2
-LAG = {1: 3, 2: 7, 3: 12, 4: 17, 5: 22, 6: 35, 7: 52, 8: 58}
+LAG = {1: 2, 2: 5, 3: 9, 4: 14, 5: 19, 6: 30, 7: 47, 8: 63}
 
 
 def dot(a, b, ca, cb):
@@ -27,7 +28,8 @@
     f = wd.shape[0]
     m = min(CHUNK, rows)
     n = rows // m
-    half, q = m // 2, m // 8
+    mp, parts = m // PARTS, n * PARTS
+    half, q = mp // 2, mp // 8
     ch, cq = d // 2, d // 4
     units, uw = n, d // n
 
@@ -77,11 +79,11 @@
 
     def send(c, k, src, dst, dev):
         return pltpu.make_async_remote_copy(
-            src, dst, ssem.at[c], rsem.at[c, k], device_id={"tp": dev}, device_id_type=MESH
+            src, dst, ssem.at[c], rsem.at[c, EVENT[k]], device_id={"tp": dev}, device_id_type=MESH
         )
 
     def place(c, h, piece):
-        return pl.ds(pl.multiple_of(c * m + h * half + piece * q, q), q)
+        return pl.ds(pl.multiple_of(c * mp + h * half + piece * q, q), q)
 
     def piece(p):
         return pl.ds(pl.multiple_of(p * q, q), q)
@@ -114,22 +116,12 @@
             return same(c, k, place(c, core, r1), hi, first[1])
         return same(c, k, place(c, core, (p1, l1, r1, o1)[k - 15]), al, partner)
 
-    def arrival(c, k):
-        if k <= 7:
-            return copy(c, k)
-        mine = place(c, core, p1)
-        if k <= 10:
-            return same(c, k, mine, cols((l2, r2, o2)[k - 8], cq), partner)
-        if k <= 12:
-            return same(c, k, place(c, core, (l1, r1)[k - 11]), al, partner)
-        if k <= 14:
-            return same(c, k, place(c, core, o1), (lo, hi)[k - 13], partner)
-        s = (p2, l2, r2, o2)[k - 15]
-        return same(c, k, place(c, 1 - core, s), al, partner)
-
-    def got(c, *ks):
-        for k in ks:
-            arrival(c, k).wait_recv()
+    arriving = ((half, d), (q, d), (2 * q, d), (q, 3 * cq), (q, 3 * cq), (2 * q, d), (q, d), (4 * q, d))
+
+    def got(c, k):
+        r, w = arriving[k - 1]
+        some = dx.at[pl.ds(0, r), pl.ds(0, w)]
+        pltpu.make_async_copy(some, some, rsem.at[c, k - 1]).wait()
 
     def go(c, *ks):
         for k in ks:
@@ -138,7 +130,7 @@
     def event(k, c):
         acc = own.at[lax.rem(c, SLOTS)]
         if k == 1:
-            got(c, 0)
+            got(c, k)
             t = acc[piece(o1), :] + rT[c, piece(o1), :].astype(F32)
             sA[c, 0] = t[:, :ch].astype(BF16)
             sA[c, 1] = t[:, ch:].astype(BF16)
@@ -146,35 +138,35 @@
                 acc[piece(p), :] = acc[piece(p), :] + rT[c, piece(p), :].astype(F32)
             go(c, 1, 2)
         elif k == 2:
-            got(c, 1, 2)
+            got(c, k)
             sB[c, 0, :, lo] = (acc[piece(r1), lo] + rA[c, 0].astype(F32)).astype(BF16)
             sB[c, 0, :, hi] = acc[piece(r1), hi].astype(BF16)
             sB[c, 1, :, lo] = acc[piece(l1), lo].astype(BF16)
             sB[c, 1, :, hi] = (acc[piece(l1), hi] + rA[c, 1].astype(F32)).astype(BF16)
             go(c, 3, 4)
         elif k == 3:
-            got(c, 3, 4)
+            got(c, k)
             acc[piece(p1), :] = acc[piece(p1), :] + rB[c, 0].astype(F32) + rB[c, 1].astype(F32)
             for i, p in enumerate((r2, l2, o2)):
                 sC[c, i] = acc[piece(p1), cols(p, cq)].astype(BF16)
             fin[c] = acc[piece(p1), cols(p2, cq)]
             go(c, 5, 6, 7)
         elif k == 4:
-            got(c, 5, 6, 7)
+            got(c, k)
             t = fin[c] + rC[c, 0].astype(F32) + rC[c, 1].astype(F32) + rC[c, 2].astype(F32)
             dx[place(c, core, p1), cols(p2, cq)] = t.astype(BF16)
             go(c, 8, 9, 10)
         elif k == 5:
-            got(c, 8, 9, 10)
+            got(c, k)
             go(c, 11, 12, 15)
         elif k == 6:
-            got(c, 11, 12)
+            got(c, k)
             go(c, 13, 14, 16, 17)
         elif k == 7:
-            got(c, 13, 14)
+            got(c, k)
             go(c, 18)
         else:
-            got(c, 15, 16, 17, 18)
+            got(c, k)
 
     c0, c1 = math.sqrt(2 / math.pi), math.sqrt(2 / math.pi) * 0.044715
 
@@ -195,15 +187,23 @@
         gu[r, w2] = (dh * act).astype(BF16)
 
     def term_part(c):
-        base = c * m
-        rp = pl.ds(pl.multiple_of(base + (1 - core) * half, half), half)
-        ro = pl.ds(pl.multiple_of(base + core * half, half), half)
-        lhs = jnp.concatenate([gu[rp, :], gu[ro, :]], 0)
+        def rows_of(s, h):
+            return gu[pl.ds(pl.multiple_of(c * m + s * mp + h * half, half), half), :]
+
+        lhs = jnp.concatenate(
+            [rows_of(s, 1 - core) for s in range(PARTS)] + [rows_of(s, core) for s in range(PARTS)], 0
+        )
         for k in range(4):
             w = pl.ds(k * cq, cq)
             t = dot(lhs, wv[w, :], 1, 1)
-            sT[c, :, w] = t[:half].astype(BF16)
-            own[lax.rem(c, SLOTS), :, w] = t[half:]
+            for s in range(PARTS):
+                p = c * PARTS + s
+                sT[p, :, w] = t[s * half : (s + 1) * half].astype(BF16)
+                own[lax.rem(p, SLOTS), :, w] = t[(PARTS + s) * half : (PARTS + s + 1) * half]
+
+    def send_term(c):
+        for s in range(PARTS):
+            go(c * PARTS + s, 0)
 
     def weights_part(j):
         r = pl.ds(pl.multiple_of(j * uw, uw), uw)
@@ -222,7 +222,7 @@
             hidden_part(c)
         else:
             term_part(c)
-            go(c, 0)
+            send_term(c)
 
             @pl.when(c + 3 < n)
             def _():
@@ -259,7 +259,7 @@
     load_wu.wait()
     term_part(0)
     pl.semaphore_wait(barrier, 6)
-    go(0, 0)
+    send_term(0)
 
     def step(t, _):
         for i in range(POINTS):
@@ -272,19 +272,20 @@
                 dw_piece(t - n, i)
 
             for k, lag in LAG.items():
-                if lag % POINTS == i:
-                    c = t - lag // POINTS
-
-                    @pl.when((c >= 0) & (c < n))
-                    def _(k=k, c=c):
-                        event(k, c)
+                for s in range(PARTS):
+                    if (lag + s) % POINTS == i:
+                        c = t - (lag + s) // POINTS
+
+                        @pl.when((c >= 0) & (c < n))
+                        def _(k=k, c=c, s=s):
+                            event(k, c * PARTS + s)
 
         return 0
 
-    lax.fori_loop(1, n + max(LAG.values()) // POINTS, step, 0)
-
-    sent = pl.ds(0, half + (2 + 1) * q + 2 * 3 * q // 4 + (2 + 1) * q + 4 * q)
-    for c in range(n):
+    lax.fori_loop(1, n + (max(LAG.values()) + PARTS - 1) // POINTS, step, 0)
+
+    sent = pl.ds(0, sum(r * w for r, w in arriving) // d)
+    for c in range(parts):
         pltpu.make_async_copy(dx.at[sent], dx.at[sent], ssem.at[c]).wait()
 
 
@@ -308,7 +309,8 @@
     def step(x, dy, gate, up, w_gate, w_up, w_down):
         (rows, d), f = x.shape, gate.shape[1]
         m = min(CHUNK, rows)
-        n, half, q = rows // m, m // 2, m // 8
+        n, mp = rows // m, m // PARTS
+        parts, half, q = n * PARTS, mp // 2, mp // 8
         vm = pltpu.VMEM
         results = pl.pallas_call(
             functools.partial(kernel, side),
@@ -317,13 +319,13 @@
             out_specs=[pl.BlockSpec(memory_space=pltpu.VMEM)] * 4,
             scratch_shapes=[
                 vm((f, d), BF16), vm((d, 2 * f), BF16), vm((rows, d), BF16), vm((rows, 2 * f), BF16), vm((rows, f), BF16),
-                vm((2, rows, d // n), BF16), vm((SLOTS, half, d), F32), vm((n, q, d // 4), F32),
-                vm((n, half, d), BF16), vm((n, half, d), BF16),
-                vm((n, 2, q, d // 2), BF16), vm((n, 2, q, d // 2), BF16),
-                vm((n, 2, q, d), BF16), vm((n, 2, q, d), BF16),
-                vm((n, 3, q, d // 4), BF16), vm((n, 3, q, d // 4), BF16),
+                vm((2, rows, d // n), BF16), vm((SLOTS, half, d), F32), vm((parts, q, d // 4), F32),
+                vm((parts, half, d), BF16), vm((parts, half, d), BF16),
+                vm((parts, 2, q, d // 2), BF16), vm((parts, 2, q, d // 2), BF16),
+                vm((parts, 2, q, d), BF16), vm((parts, 2, q, d), BF16),
+                vm((parts, 3, q, d // 4), BF16), vm((parts, 3, q, d // 4), BF16),
                 pltpu.SemaphoreType.DMA((3,)), pltpu.SemaphoreType.DMA((n, 3)), pltpu.SemaphoreType.DMA((2,)),
-                pltpu.SemaphoreType.DMA((n,)), pltpu.SemaphoreType.DMA((n, COPIES)),
+                pltpu.SemaphoreType.DMA((parts,)), pltpu.SemaphoreType.DMA((parts, 8)),
             ],
             compiler_params=pltpu.CompilerParams(
                 collective_id=0, has_side_effects=True, vmem_limit_bytes=49 * 2**20 + 2**19

time: 73.6 us -> 72.1 us (0.980)
  Pallas kernels: 72.8 us -> 71.4 us
    pallas_call x1, Pallas kernels: 67.5 us -> 66.1 us  [step(): pl.pallas_call(functools.partial(kernel, side), out_shape=[vm((rows, d),...]
where the time goes in v4:
time: 72.1 us; the launch traced here: 72 us
  Pallas kernels  71.4 us (99%)
    pallas_call x1, Pallas kernels, step(): pl.pallas_call(functools.partial(kernel, side), out_shape=[vm((rows, d),...  66.1 us
    pallas_call x1, Pallas kernels, step(): pl.pallas_call(flush, out_shape=[jax.ShapeDtypeStruct(a.shape, a.dtype) f...  5.32 us

profile of v4, /device:TPU:97, one launch (start us, length us, event | category | flops | bytes accessed | tf_op | source)
XLA Modules:
  0.0 72.0 jit_solution(10811441428387936666)
XLA Ops:
  0.6 66.1 %shard_map.102 = (bf16[2048,2048]{1,0:T(8,128)(2,1)S(1)}, bf16[2048,512]{1,0:T(8,128)(2,1)S(1)}, bf16[2048,512]{1,0:T(8,128)(2,1)S(1)}, bf16[512,2048]{1,0:T(8,128)(2,1)S(1)}) custom-call(bf16[2048,2048]{1,0:T(8,128)(2,1)} %x.1, bf16[2048,2048]{1,0:T(8,128)(2,1)} %dy.1, bf16[2048,512]{1,0:T(8,128)(2,1)} %gate.1, bf16[2048,512]{1,0:T(8,128)(2,1)} %up.1, ...), custom_call_target="tpu_custom_call" | custom-call | tf_op jit(solution)/shard_map/pallas_call | solution.py:315
  66.7 5.3 %shard_map.103 = (bf16[2048,2048]{1,0:T(8,128)(2,1)}, bf16[2048,512]{1,0:T(8,128)(2,1)}, bf16[2048,512]{1,0:T(8,128)(2,1)}, bf16[512,2048]{1,0:T(8,128)(2,1)}) custom-call(bf16[2048,2048]{1,0:T(8,128)(2,1)S(1)} %get-tuple-element.8.refs_0_, bf16[2048,512]{1,0:T(8,128)(2,1)S(1)} %get-tuple-element.9.refs_1_, bf16[2048,512]{1,0:T(8,128)(2,1)S(1)} %get-tuple-element.10.refs_2_, ...), custom_call_target="tpu_custom_call" | custom-call | tf_op jit(solution)/shard_map/pallas_call | solution.py:334

commit v5 on v4

--- a/solution.py
+++ b/solution.py
@@ -15,7 +15,7 @@
 EVENT = (0, 1, 1, 2, 2, 3, 3, 3, 4, 4, 4, 5, 5, 6, 6, 7, 7, 7, 7)
 SLOTS = 12
 POINTS = 2
-LAG = {1: 2, 2: 5, 3: 9, 4: 14, 5: 19, 6: 30, 7: 47, 8: 63}
+LAG = {1: 2, 2: 5, 3: 9, 4: 14, 5: 19, 6: 30, 7: 47}
 
 
 def dot(a, b, ca, cb):
@@ -23,7 +23,7 @@
 
 
 def kernel(side, x, dy, gate, up, wg, wu, wd, dx, dwg, dwu, dwd,
-           wdv, wv, dyv, gu, hid, xs, own, fin, sT, rT, sA, rA, sB, rB, sC, rC, wsem, lsem, xsem, ssem, rsem):
+           wdv, wv, dyv, gu, hid, xs, own, fin, sT, rT, sA, rA, sB, rB, sC, rC, wsem, lsem, xsem, ssem, rsem, psem):
     rows, d = dx.shape
     f = wd.shape[0]
     m = min(CHUNK, rows)
@@ -62,9 +62,9 @@
     def chunk_loads(c):
         r = pl.ds(pl.multiple_of(c * m, m), m)
         return (
-            load(dy.at[r], dyv.at[r], lsem.at[c, 0]),
-            load(gate.at[r], gu.at[r, pl.ds(0, f)], lsem.at[c, 1]),
-            load(up.at[r], gu.at[r, pl.ds(f, f)], lsem.at[c, 2]),
+            load(dy.at[r], dyv.at[r], lsem.at[lax.rem(c, 4), 0]),
+            load(gate.at[r], gu.at[r, pl.ds(0, f)], lsem.at[lax.rem(c, 4), 1]),
+            load(up.at[r], gu.at[r, pl.ds(f, f)], lsem.at[lax.rem(c, 4), 2]),
         )
 
     def unit_load(j, slot):
@@ -78,8 +78,9 @@
         cp.start()
 
     def send(c, k, src, dst, dev):
+        arrived = rsem.at[c, EVENT[k]] if EVENT[k] < 7 else psem.at[0]
         return pltpu.make_async_remote_copy(
-            src, dst, ssem.at[c], rsem.at[c, EVENT[k]], device_id={"tp": dev}, device_id_type=MESH
+            src, dst, ssem.at[lax.div(c, parts // 2)], arrived, device_id={"tp": dev}, device_id_type=MESH
         )
 
     def place(c, h, piece):
@@ -118,10 +119,13 @@
 
     arriving = ((half, d), (q, d), (2 * q, d), (q, 3 * cq), (q, 3 * cq), (2 * q, d), (q, d), (4 * q, d))
 
+    def take(sem, r, w):
+        some = dx.at[pl.ds(0, r), pl.ds(0, w)]
+        pltpu.make_async_copy(some, some, sem).wait()
+
     def got(c, k):
         r, w = arriving[k - 1]
-        some = dx.at[pl.ds(0, r), pl.ds(0, w)]
-        pltpu.make_async_copy(some, some, rsem.at[c, k - 1]).wait()
+        take(rsem.at[c, k - 1], r, w)
 
     def go(c, *ks):
         for k in ks:
@@ -130,7 +134,6 @@
     def event(k, c):
         acc = own.at[lax.rem(c, SLOTS)]
         if k == 1:
-            got(c, k)
             t = acc[piece(o1), :] + rT[c, piece(o1), :].astype(F32)
             sA[c, 0] = t[:, :ch].astype(BF16)
             sA[c, 1] = t[:, ch:].astype(BF16)
@@ -138,35 +141,27 @@
                 acc[piece(p), :] = acc[piece(p), :] + rT[c, piece(p), :].astype(F32)
             go(c, 1, 2)
         elif k == 2:
-            got(c, k)
             sB[c, 0, :, lo] = (acc[piece(r1), lo] + rA[c, 0].astype(F32)).astype(BF16)
             sB[c, 0, :, hi] = acc[piece(r1), hi].astype(BF16)
             sB[c, 1, :, lo] = acc[piece(l1), lo].astype(BF16)
             sB[c, 1, :, hi] = (acc[piece(l1), hi] + rA[c, 1].astype(F32)).astype(BF16)
             go(c, 3, 4)
         elif k == 3:
-            got(c, k)
             acc[piece(p1), :] = acc[piece(p1), :] + rB[c, 0].astype(F32) + rB[c, 1].astype(F32)
             for i, p in enumerate((r2, l2, o2)):
                 sC[c, i] = acc[piece(p1), cols(p, cq)].astype(BF16)
             fin[c] = acc[piece(p1), cols(p2, cq)]
             go(c, 5, 6, 7)
         elif k == 4:
-            got(c, k)
             t = fin[c] + rC[c, 0].astype(F32) + rC[c, 1].astype(F32) + rC[c, 2].astype(F32)
             dx[place(c, core, p1), cols(p2, cq)] = t.astype(BF16)
             go(c, 8, 9, 10)
         elif k == 5:
-            got(c, k)
             go(c, 11, 12, 15)
         elif k == 6:
-            got(c, k)
             go(c, 13, 14, 16, 17)
-        elif k == 7:
-            got(c, k)
+        else:
             go(c, 18)
-        else:
-            got(c, k)
 
     c0, c1 = math.sqrt(2 / math.pi), math.sqrt(2 / math.pi) * 0.044715
 
@@ -278,15 +273,16 @@
 
                         @pl.when((c >= 0) & (c < n))
                         def _(k=k, c=c, s=s):
+                            got(c * PARTS + s, k)
                             event(k, c * PARTS + s)
 
         return 0
 
     lax.fori_loop(1, n + (max(LAG.values()) + PARTS - 1) // POINTS, step, 0)
 
-    sent = pl.ds(0, sum(r * w for r, w in arriving) // d)
-    for c in range(parts):
-        pltpu.make_async_copy(dx.at[sent], dx.at[sent], ssem.at[c]).wait()
+    take(psem.at[0], parts * arriving[7][0], d)
+    for i in range(2):
+        take(ssem.at[i], parts // 2 * sum(r * w for r, w in arriving) // d, d)
 
 
 def flush(*refs):
@@ -324,8 +320,8 @@
                 vm((parts, 2, q, d // 2), BF16), vm((parts, 2, q, d // 2), BF16),
                 vm((parts, 2, q, d), BF16), vm((parts, 2, q, d), BF16),
                 vm((parts, 3, q, d // 4), BF16), vm((parts, 3, q, d // 4), BF16),
-                pltpu.SemaphoreType.DMA((3,)), pltpu.SemaphoreType.DMA((n, 3)), pltpu.SemaphoreType.DMA((2,)),
-                pltpu.SemaphoreType.DMA((parts,)), pltpu.SemaphoreType.DMA((parts, 8)),
+                pltpu.SemaphoreType.DMA((3,)), pltpu.SemaphoreType.DMA((4, 3)), pltpu.SemaphoreType.DMA((2,)),
+                pltpu.SemaphoreType.DMA((2,)), pltpu.SemaphoreType.DMA((parts, 7)), pltpu.SemaphoreType.DMA((1,)),
             ],
             compiler_params=pltpu.CompilerParams(
                 collective_id=0, has_side_effects=True, vmem_limit_bytes=49 * 2**20 + 2**19

time: 72.1 us -> 71.6 us (level)
  no operation moved by 1% of the time
where the time goes in v5:
time: 71.6 us; the launch traced here: 71.5 us
  Pallas kernels  70.9 us (99%)
    pallas_call x1, Pallas kernels, step(): pl.pallas_call(functools.partial(kernel, side), out_shape=[vm((rows, d),...  65.6 us
    pallas_call x1, Pallas kernels, step(): pl.pallas_call(flush, out_shape=[jax.ShapeDtypeStruct(a.shape, a.dtype) f...  5.32 us

profile of v5, /device:TPU:97, one launch (start us, length us, event | category | flops | bytes accessed | tf_op | source)
XLA Modules:
  0.0 71.5 jit_solution(12281178495485430401)
XLA Ops:
  0.6 65.6 %shard_map.102 = (bf16[2048,2048]{1,0:T(8,128)(2,1)S(1)}, bf16[2048,512]{1,0:T(8,128)(2,1)S(1)}, bf16[2048,512]{1,0:T(8,128)(2,1)S(1)}, bf16[512,2048]{1,0:T(8,128)(2,1)S(1)}) custom-call(bf16[2048,2048]{1,0:T(8,128)(2,1)} %x.1, bf16[2048,2048]{1,0:T(8,128)(2,1)} %dy.1, bf16[2048,512]{1,0:T(8,128)(2,1)} %gate.1, bf16[2048,512]{1,0:T(8,128)(2,1)} %up.1, ...), custom_call_target="tpu_custom_call" | custom-call | tf_op jit(solution)/shard_map/pallas_call | solution.py:311
  66.2 5.3 %shard_map.103 = (bf16[2048,2048]{1,0:T(8,128)(2,1)}, bf16[2048,512]{1,0:T(8,128)(2,1)}, bf16[2048,512]{1,0:T(8,128)(2,1)}, bf16[512,2048]{1,0:T(8,128)(2,1)}) custom-call(bf16[2048,2048]{1,0:T(8,128)(2,1)S(1)} %get-tuple-element.8.refs_0_, bf16[2048,512]{1,0:T(8,128)(2,1)S(1)} %get-tuple-element.9.refs_1_, bf16[2048,512]{1,0:T(8,128)(2,1)S(1)} %get-tuple-element.10.refs_2_, ...), custom_call_target="tpu_custom_call" | custom-call | tf_op jit(solution)/shard_map/pallas_call | solution.py:330
